TPU v7x, 256 devices: a whole 4x4x8 slice. The times are simulated.
256 devices in a mesh: lat: 32 (over y_hi, z, core), lon: 8 (over y_lo, x).
Axes of the slice: x: 4, y: 4 (y_hi: 2, y_lo: 2; y = y_hi * 2 + y_lo), z: 8, core: 2. Of those that a mesh axis runs over, the one named last changes fastest.
Arguments:
- field: bfloat16 [384, 768, 512], P('lat', 'lon'), may hold values from -6 to 6
- quad_weight: float32 [384], P('lat'), may hold values from 0.5 to 1.5
- legendre: bfloat16 [384, 384, 384], P('lat'), as said below
- filter_real: float32 [384, 512], replicated, may hold values from -4 to 4
- filter_imag: float32 [384, 512], replicated, may hold values from -4 to 4
- neighbour: int32 [384, 12], P('lat'), may hold values from 0 to 24
- basis: int32 [384, 12], P('lat'), may hold values from 0 to 7
- disco_quad: float32 [384, 12], P('lat'), may hold values from 0.5 to 1.5
- disco_weight: float32 [8, 512], replicated, may hold values from -2 to 2
- norm_gain: float32 [512], replicated, may hold values from 0.5 to 1.5
- w_in: bfloat16 [512, 1024], replicated, may hold values from -0.25 to 0.25
- b_in: float32 [1024], replicated, may hold values from -3 to 3
- w_out: bfloat16 [1024, 512], replicated, may hold values from -0.1875 to 0.1875
- b_out: float32 [512], replicated, may hold values from -3 to 3
Outputs:
- block_out: bfloat16 [384, 768, 512], P('lat', 'lon')
- spatial: bfloat16 [384, 768, 512], P('lat', 'lon')
Inputs may be any that keep to these rules, and one draw needn't show every extreme that they name: legendre[m, l, t] = 0 for l < m.
All inputs are finite; a program needn't handle non-finite values.
Results may differ from a plain program's by a relative error of at most 0.018.
Values may be sent and summed in bfloat16 or wider, within the bound.
A program may use at most 64 MiB of HBM per device.

v0:
```python
import math
import jax
import jax.numpy as jnp
from jax import lax
from jax.sharding import PartitionSpec as P

HALO = 2
KB = 8
NWIN = 25
exact_mode = lax.Precision.HIGHEST


def padded_2(block, sides, width):
    for axis, dim in sides:
        count = lax.axis_size(axis)
        forward = [(i, i + 1) for i in range(count - 1)]
        backward = [(target, source) for source, target in forward]
        low = lax.ppermute(
            lax.slice_in_dim(block, block.shape[dim] - width, None, axis=dim), axis, forward
        )
        high = lax.ppermute(lax.slice_in_dim(block, 0, width, axis=dim), axis, backward)
        block = jnp.concatenate([low, block, high], axis=dim)
    return block


def split_table(table):
    upper = table.astype(jnp.bfloat16)
    lower = (table - upper.astype(jnp.float32)).astype(jnp.bfloat16)
    return (upper, lower)


def fourier_tables(nlon, mmax):
    points = jnp.arange(nlon, dtype=jnp.int32)
    waves = jnp.arange(mmax, dtype=jnp.int32)
    phase = waves[:, None] * points[None, :] % nlon
    angle = phase.astype(jnp.float32) * (2.0 * math.pi / nlon)
    cosine = jnp.cos(angle) / math.sqrt(nlon)
    sine = jnp.sin(angle) / math.sqrt(nlon)
    forward_table = jnp.stack([cosine, -sine], axis=0)
    factor = jnp.where(waves == 0, 1.0, 2.0).astype(jnp.float32)[:, None]
    inverse_table = jnp.stack([factor * cosine, -factor * sine], axis=0)
    return (forward_table, inverse_table)


def window_kernel(neighbour, basis, disco_quad, weight_cols):
    places = (neighbour[:, :, None] == jnp.arange(NWIN, dtype=jnp.int32)[None, None, :]).astype(
        jnp.float32
    )
    places = places * disco_quad[:, :, None]
    kinds = (basis[:, :, None] == jnp.arange(KB, dtype=jnp.int32)[None, None, :]).astype(
        jnp.float32
    )
    mixing = jnp.einsum("isn,isb->inb", places, kinds, precision=exact_mode)
    return jnp.einsum("inb,bc->inc", mixing, weight_cols, precision=exact_mode)


def convolve(padded, kernel, lat_rows, lon_cols):
    span = 2 * HALO + 1
    total = jnp.zeros((lat_rows, lon_cols, kernel.shape[2]), jnp.float32)
    for offset in range(NWIN):
        row_shift = offset // span
        col_shift = offset % span
        window = padded[row_shift : row_shift + lat_rows, col_shift : col_shift + lon_cols, :]
        total = total + kernel[:, offset, None, :] * window
    return total


def channel_mlp(spatial, field, norm_gain, w_in, b_in, w_out, b_out):
    channels = spatial.shape[-1]
    tokens = spatial.reshape(-1, channels).astype(jnp.float32)
    center = jnp.mean(tokens, axis=1, keepdims=True)
    spread = jnp.mean((tokens - center) ** 2, axis=1, keepdims=True)
    normed = ((tokens - center) * lax.rsqrt(spread + 1e-05) * norm_gain).astype(jnp.bfloat16)
    hidden = jnp.dot(normed, w_in, preferred_element_type=jnp.float32) + b_in
    hidden = jax.nn.gelu(hidden).astype(jnp.bfloat16)
    result = jnp.dot(hidden, w_out, preferred_element_type=jnp.float32)
    result = result + b_out + field.reshape(-1, channels).astype(jnp.float32)
    return result.astype(jnp.bfloat16).reshape(field.shape)


def shards(
    field,
    quad_weight,
    legendre,
    filter_real,
    filter_imag,
    neighbour,
    basis,
    disco_quad,
    disco_weight,
    norm_gain,
    w_in,
    b_in,
    w_out,
    b_out,
):
    lat_rows, lon_cols, channels = field.shape
    lon_count = lax.axis_size("lon")
    lat_count = lax.axis_size("lat")
    nlon = lon_cols * lon_count
    wave_block = legendre.shape[0]
    mmax = wave_block * lat_count
    cblock = channels // lon_count
    forward_table, inverse_table = fourier_tables(nlon, mmax)
    forward_upper, forward_lower = split_table(forward_table)
    inverse_upper, inverse_lower = split_table(inverse_table)
    columns = lax.all_to_all(field, "lon", split_axis=2, concat_axis=1, tiled=True)
    frequency = jnp.einsum(
        "tkc,rmk->rmtc", columns, forward_upper, preferred_element_type=jnp.float32
    )
    frequency = frequency + jnp.einsum(
        "tkc,rmk->rmtc", columns, forward_lower, preferred_element_type=jnp.float32
    )
    weighted = (frequency * quad_weight[None, None, :, None]).astype(jnp.bfloat16)
    weighted = jnp.transpose(weighted, (1, 2, 0, 3))
    coeffs = jnp.einsum(
        "mlt,mtrc->mlrc",
        legendre,
        lax.all_to_all(weighted, "lat", split_axis=0, concat_axis=1, tiled=True),
        preferred_element_type=jnp.float32,
    )
    chan_start = lax.axis_index("lon") * cblock
    gain_real = lax.dynamic_slice_in_dim(filter_real, chan_start, cblock, 1)[None, :, :]
    gain_imag = lax.dynamic_slice_in_dim(filter_imag, chan_start, cblock, 1)[None, :, :]
    real_part = coeffs[:, :, 0]
    imag_part = coeffs[:, :, 1]
    filtered = jnp.stack(
        [
            gain_real * real_part - gain_imag * imag_part,
            gain_real * imag_part + gain_imag * real_part,
        ],
        axis=2,
    ).astype(jnp.bfloat16)
    synthesis = jnp.einsum(
        "mlt,mlrc->mtrc", legendre, filtered, preferred_element_type=jnp.float32
    ).astype(jnp.bfloat16)
    lat_block = lax.all_to_all(synthesis, "lat", split_axis=1, concat_axis=0, tiled=True)
    wave = jnp.einsum("mtrc,rmk->tkc", lat_block, inverse_upper, preferred_element_type=jnp.float32)
    wave = wave + jnp.einsum(
        "mtrc,rmk->tkc", lat_block, inverse_lower, preferred_element_type=jnp.float32
    )
    wave = wave.astype(jnp.bfloat16)
    weight_cols = lax.dynamic_slice_in_dim(disco_weight, chan_start, cblock, 1)
    kernel = window_kernel(neighbour, basis, disco_quad, weight_cols)
    cycle = jnp.concatenate([wave[:, nlon - HALO :], wave, wave[:, :HALO]], axis=1)
    padded = padded_2(cycle, (("lat", 0),), HALO)
    conv = convolve(padded, kernel, lat_rows, nlon)
    spatial_part = (wave.astype(jnp.float32) + conv).astype(jnp.bfloat16)
    spatial = lax.all_to_all(spatial_part, "lon", split_axis=1, concat_axis=2, tiled=True)
    block_out = channel_mlp(spatial, field, norm_gain, w_in, b_in, w_out, b_out)
    return (block_out, spatial)


def solution(mesh):
    placed = (
        P("lat", "lon", None),
        P("lat"),
        P("lat", None, None),
        P(),
        P(),
        P("lat", None),
        P("lat", None),
        P("lat", None),
        P(),
        P(),
        P(),
        P(),
        P(),
        P(),
    )
    return jax.shard_map(
        shards,
        mesh=mesh,
        in_specs=placed,
        out_specs=(P("lat", "lon", None), P("lat", "lon", None)),
        check_vma=False,
    )
```

profile of v0, /device:TPU:16, one launch (start us, length us, event | category | flops | bytes accessed | tf_op | source)
XLA Modules:
  0.0 266.1 jit_solution(6598086077392066688)
XLA Ops:
  0.6 4.5 %copy.55 = bf16[12,96,512]{1,0,2:T(8,128)(2,1)} copy(bf16[12,96,512]{2,1,0:T(8,128)(2,1)} %param.14) | data formatting | bytes 2359296 | tf_op args[0]
  5.1 5.0 %all-to-all-start = ((bf16[12,96,512]{1,0,2:T(8,128)(2,1)}), bf16[12,96,512]{1,0,2:T(8,128)(2,1)}, u32[]{:S(2)}, u32[]{:S(2)}) async-start(bf16[12,96,512]{1,0,2:T(8,128)(2,1)} %copy.55), calls=%async_computation | async-start | bytes 4194304 | tf_op jit(solution)/shard_map/all_to_all | solution.py:107
  10.2 6.4 %multiply_negate_fusion = (f32[1,384,768]{2,1,0:T(8,128)}, f32[1,384,768]{2,1,0:T(8,128)}) fusion(), kind=kLoop, calls=%fused_computation.79 | loop fusion | flops 3538944 | bytes 2359296 | tf_op jit(solution)/shard_map/neg | solution.py:39
  16.5 20.7 %all-to-all-done = bf16[12,96,512]{1,0,2:T(8,128)(2,1)} async-done(((bf16[12,96,512]{1,0,2:T(8,128)(2,1)}), bf16[12,96,512]{1,0,2:T(8,128)(2,1)}, u32[]{:S(2)}, u32[]{:S(2)}) %all-to-all-start) | async-done | bytes 1179680 | tf_op jit(solution)/shard_map/all_to_all | solution.py:107
  37.2 3.8 %copy.57 = bf16[12,8,96,64]{2,1,3,0:T(8,128)(2,1)} copy(bf16[12,8,96,64]{2,0,3,1:T(8,128)(2,1)} %bitcast.4) | data formatting | bytes 2359296 | tf_op jit(solution)/shard_map/all_to_all | solution.py:107
  41.0 3.8 %reshape.182 = bf16[12,768,64,1]{1,2,0,3:T(8,128)(2,1)} reshape(bf16[12,8,96,64]{2,1,3,0:T(8,128)(2,1)} %copy.57) | data formatting | bytes 2359296 | tf_op jit(solution)/shard_map/all_to_all | solution.py:107
  44.8 3.2 %fusion.48 = f32[2,384,12,64]{1,3,2,0:T(8,128)S(1)} fusion(bf16[12,768,64,1]{1,2,0,3:T(8,128)(2,1)} %reshape.182, f32[1,384,768]{2,1,0:T(8,128)} %get-tuple-element.41, f32[1,384,768]{2,1,0:T(8,128)} %get-tuple-element.42), kind=kOutput, calls=%fused_computation.61 | convolution fusion | flops 908328960 | bytes 5898240 | tf_op jit(solution)/shard_map/tkc,rmk->rmtc/dot_general | solution.py:108
  48.1 2.2 fusion.41
  50.3 6.7 %copy.58 = bf16[384,12,2,64]{3,2,1,0:T(2,128)(2,1)} copy(bf16[384,12,2,64]{0,3,1,2:T(8,128)(2,1)} %fusion.41) | data formatting | bytes 2359296 | tf_op jit(solution)/shard_map/convert_element_type | solution.py:114
  56.9 6.3 %reshape.191 = bf16[32,2,9216]{2,1,0:T(2,128)(2,1)} reshape(bf16[384,12,2,64]{3,2,1,0:T(2,128)(2,1)} %copy.58) | data formatting | bytes 2359296
  63.2 11.8 %all-to-all-start.1 = ((bf16[32,2,9216]{2,1,0:T(2,128)(2,1)}), bf16[32,2,9216]{2,1,0:T(2,128)(2,1)}, u32[]{:S(2)}, u32[]{:S(2)}) async-start(bf16[32,2,9216]{2,1,0:T(2,128)(2,1)} %reshape.191), calls=%async_computation.1 | async-start | bytes 2359296 | tf_op jit(solution)/shard_map/all_to_all | solution.py:119
  75.0 2.0 constant_dynamic-slice_fusion
  77.0 1.7 copy.61
  78.7 1.7 copy.54
  80.3 1.0 fusion.74
  81.3 1.2 fusion.80
  82.6 0.7 copy-done.8
  83.2 0.7 fusion.96
  83.9 0.6 copy.132
  84.5 0.6 select_multiply_fusion
  85.1 0.6 fusion.83
  85.7 0.6 copy_bitcast_fusion.2
  86.3 0.6 copy_bitcast_fusion.4
  86.9 17.9 %all-to-all-done.1 = bf16[32,2,9216]{2,1,0:T(2,128)(2,1)} async-done(((bf16[32,2,9216]{2,1,0:T(2,128)(2,1)}), bf16[32,2,9216]{2,1,0:T(2,128)(2,1)}, u32[]{:S(2)}, u32[]{:S(2)}) %all-to-all-start.1) | async-done | bytes 1179680 | tf_op jit(solution)/shard_map/all_to_all | solution.py:119
  104.8 6.3 %reshape.192 = bf16[384,12,2,64]{3,2,1,0:T(2,128)(2,1)} reshape(bf16[32,2,9216]{2,1,0:T(2,128)(2,1)} %all-to-all-done.1) | data formatting | bytes 2359296
  111.1 3.7 %copy.59 = bf16[12,32,12,2,64]{4,3,2,1,0:T(2,128)(2,1)S(1)} copy(bf16[12,32,12,2,64]{4,3,2,0,1:T(2,128)(2,1)} %bitcast.148) | data formatting | bytes 2359296 | tf_op jit(solution)/shard_map/all_to_all | solution.py:119
  114.8 1.6 fusion.32
  116.8 2.0 fusion.43
  118.8 5.6 %copy.62 = bf16[12,384,2,64]{3,2,0,1:T(2,128)(2,1)S(1)} copy(bf16[12,384,2,64]{1,3,2,0:T(8,128)(2,1)} %fusion.43) | data formatting | bytes 2359296 | tf_op jit(solution)/shard_map/convert_element_type | solution.py:136
  124.4 2.2 reshape.193
  126.7 7.1 %all-to-all-start.2 = ((bf16[32,2,9216]{2,1,0:T(2,128)(2,1)}), bf16[32,2,9216]{2,1,0:T(2,128)(2,1)S(1)}, u32[]{:S(2)}, u32[]{:S(2)}) async-start(bf16[32,2,9216]{2,1,0:T(2,128)(2,1)} %reshape.193), calls=%async_computation.2 | async-start | bytes 2359296 | tf_op jit(solution)/shard_map/all_to_all | solution.py:137
  133.9 0.6 copy_bitcast_fusion.6
  134.5 0.6 copy_bitcast_fusion.8
  135.1 0.6 copy_bitcast_fusion.10
  135.7 0.6 copy_bitcast_fusion.12
  136.3 0.6 copy_bitcast_fusion.14
  136.9 0.6 copy_bitcast_fusion.16
  137.6 2.1 fusion.97
  139.6 0.6 copy_bitcast_fusion.18
  140.2 0.6 copy_bitcast_fusion.20
  140.8 6.0 %fusion.71 = (f32[1,384,768]{2,1,0:T(8,128)}, f32[1,384,768]{2,1,0:T(8,128)}) fusion(f32[384]{0:T(512)S(1)} %copy-done.46, f32[384]{0:T(512)S(1)} %copy-done.47), kind=kLoop, calls=%fused_computation.86 | loop fusion | flops 3244032 | bytes 2362368 | tf_op jit(solution)/shard_map/mul | solution.py:41
  146.8 16.7 %all-to-all-done.2 = bf16[32,2,9216]{2,1,0:T(2,128)(2,1)S(1)} async-done(((bf16[32,2,9216]{2,1,0:T(2,128)(2,1)}), bf16[32,2,9216]{2,1,0:T(2,128)(2,1)S(1)}, u32[]{:S(2)}, u32[]{:S(2)}) %all-to-all-start.2) | async-done | bytes 1179680 | tf_op jit(solution)/shard_map/all_to_all | solution.py:137
  163.5 1.4 reshape.194
  164.9 3.0 %copy.64 = bf16[32,12,12,2,64]{4,3,2,1,0:T(2,128)(2,1)} copy(bf16[32,12,12,2,64]{4,3,1,2,0:T(2,128)(2,1)S(1)} %bitcast.150) | data formatting | bytes 2359296 | tf_op jit(solution)/shard_map/all_to_all | solution.py:137
  167.9 5.9 %copy.65 = bf16[384,12,2,64]{0,3,2,1:T(8,128)(2,1)S(1)} copy(bf16[384,12,2,64]{3,2,1,0:T(2,128)(2,1)} %bitcast.151) | data formatting | bytes 2359296 | tf_op jit(solution)/shard_map/all_to_all | solution.py:137
  173.8 1.1 fusion.50
  175.1 1.2 fusion.42
  176.7 1.9 collective-permute-start
  178.6 7.3 %collective-permute-start.1 = (bf16[2,772,64]{1,2,0:T(8,128)(2,1)S(1)}, bf16[2,772,64]{1,2,0:T(8,128)(2,1)S(1)}, u32[]{:S(2)}, u32[]{:S(2)}) collective-permute-start(bf16[2,772,64]{1,2,0:T(8,128)(2,1)S(1)} %get-tuple-element.13), channel_id=1, source_target_pairs={{8,0},{16,8},{24,16},{32,24},{40,32},{48,40},{56,48},{64,56},{72,6... | collective-permute-start | bytes 592904 | tf_op jit(solution)/shard_map/ppermute | solution.py:21
  186.1 1.5 collective-permute-done
  187.6 1.8 collective-permute-done.1
  189.4 2.0 maximum_maximum_fusion
  191.6 15.5 %fusion.29 = bf16[12,768,64]{1,2,0:T(8,128)(2,1)} fusion(bf16[12,768,64]{1,2,0:T(8,128)(2,1)S(1)} %fusion.42, bf16[12,2,64]{1,2,0:T(8,128)(2,1)S(1)} %get-tuple-element.15, bf16[12,2,64]{1,2,0:T(8,128)(2,1)S(1)} %get-tuple-element.14, bf16[14,772,64]{1,2,0:T(8,128)(2,1)S(1)} %get-tuple-element.11, bf16[14,772,64]{1,2,0:T(8,128)(2,1)S(1)} %get-tuple-element.10, ...), kind=kLoop, calls=%fused_computation.42 | loop fusion | flops 51904512 | bytes 26035200 | tf_op jit(solution)/shard_map/convert_element_type | solution.py:148
  207.1 3.9 %copy.67 = bf16[12,768,64]{2,0,1:T(8,128)(2,1)S(1)} copy(bf16[12,768,64]{1,2,0:T(8,128)(2,1)} %fusion.29) | data formatting | bytes 2359296 | tf_op jit(solution)/shard_map/convert_element_type | solution.py:148
  211.0 2.9 %reshape.195 = bf16[8,2,36864]{2,1,0:T(2,128)(2,1)} reshape(bf16[768,12,64]{2,1,0:T(8,128)(2,1)S(1)} %bitcast.147) | data formatting | bytes 2359296
  213.9 22.6 %all_to_all.72 = bf16[8,2,36864]{2,1,0:T(2,128)(2,1)S(1)} all-to-all(bf16[8,2,36864]{2,1,0:T(2,128)(2,1)} %reshape.195), channel_id=1, replica_groups=mesh['lat'=32,'lon'=8] {'lon'}, dimensions={0} | all-to-all | bytes 2359296 | tf_op jit(solution)/shard_map/all_to_all | solution.py:149
  236.5 3.2 %reshape.196 = bf16[768,12,64]{2,1,0:T(8,128)(2,1)} reshape(bf16[8,2,36864]{2,1,0:T(2,128)(2,1)S(1)} %all_to_all.72) | data formatting | bytes 2359296
  239.7 3.9 %copy.68 = bf16[12,8,96,64]{2,3,1,0:T(8,128)(2,1)S(1)} copy(bf16[12,8,96,64]{3,0,2,1:T(8,128)(2,1)} %bitcast.146) | data formatting | bytes 2359296 | tf_op jit(solution)/shard_map/all_to_all | solution.py:149
  243.5 2.1 bitcast_convert_fusion
  245.9 0.5 multiply_reduce_fusion
  246.5 5.7 %copy.69 = f32[12,96,8,64]{1,0,3,2:T(8,128)} copy(f32[12,96,8,64]{1,3,2,0:T(8,128)} %bitcast_convert_fusion) | data formatting | bytes 4718592 | tf_op jit(solution)/shard_map/convert_element_type | solution.py:70
  252.2 5.1 %reshape.179 = f32[1152,512]{0,1:T(8,128)} reshape(f32[12,96,8,64]{1,0,3,2:T(8,128)} %copy.69) | data formatting | bytes 4718592 | tf_op jit(solution)/shard_map/convert_element_type | solution.py:70
  257.4 1.5 copy.70
  258.9 7.2 %fusion.13 = bf16[1152,512]{1,0:T(8,128)(2,1)} fusion(bf16[1024,512]{1,0:T(8,128)(2,1)} %param.26, bf16[1152,512]{1,0:T(8,128)(2,1)} %bitcast.153, f32[512]{0:T(512)} %param.27, bf16[512,1024]{1,0:T(8,128)(2,1)} %param.24, f32[1024]{0:T(1024)} %param.25, f32[1152,512]{0,1:T(8,128)} %reshape.179, f32[512]{0:T(512)} %param.23, f32[1152]{0:T(1024)S(1)} %rsqrt.12, ...), kind=kOutput, calls=%fused_computation.17 | convolution fusion | flops 2432434176 | bytes 6833152 | tf_op jit(solution)/shard_map/dot_general | solution.py:76
  (111 shorter events, 1.6 us)
Async XLA Ops:
  0.6 114.1 %copy-start = (bf16[12,384,384]{2,1,0:T(8,128)(2,1)S(1)}, bf16[12,384,384]{2,1,0:T(8,128)(2,1)}, u32[]{:S(2)}) copy-start(bf16[12,384,384]{2,1,0:T(8,128)(2,1)} %param.16) | copy-start | bytes 10616836
  5.1 32.1 %all-to-all-start = ((bf16[12,96,512]{1,0,2:T(8,128)(2,1)}), bf16[12,96,512]{1,0,2:T(8,128)(2,1)}, u32[]{:S(2)}, u32[]{:S(2)}) async-start(bf16[12,96,512]{1,0,2:T(8,128)(2,1)} %copy.55), calls=%async_computation | async-start | bytes 4194304 | tf_op jit(solution)/shard_map/all_to_all | solution.py:107
  44.8 3.3 %copy-start.5 = (f32[1,384,768]{2,1,0:T(8,128)S(1)}, f32[1,384,768]{2,1,0:T(8,128)}, u32[]{:S(2)}) copy-start(f32[1,384,768]{2,1,0:T(8,128)} %get-tuple-element.41) | copy-start | bytes 3538948
  44.8 3.3 %copy-start.6 = (f32[1,384,768]{2,1,0:T(8,128)S(1)}, f32[1,384,768]{2,1,0:T(8,128)}, u32[]{:S(2)}) copy-start(f32[1,384,768]{2,1,0:T(8,128)} %get-tuple-element.42) | copy-start | bytes 3538948
  44.8 3.3 %copy-start.7 = (bf16[12,768,64,1]{1,2,0,3:T(8,128)(2,1)S(1)}, bf16[12,768,64,1]{1,2,0,3:T(8,128)(2,1)}, u32[]{:S(2)}) copy-start(bf16[12,768,64,1]{1,2,0,3:T(8,128)(2,1)} %reshape.182) | copy-start | bytes 3538948
  44.8 3.3 %copy-start.50 = (f32[12]{0:T(128)S(1)}, f32[12]{0:T(128)}, u32[]{:S(2)}) copy-start(f32[12]{0:T(128)} %param.15) | copy-start | bytes 148
  63.2 17.1 %copy-start.48 = (f32[12,12]{1,0:T(8,128)S(1)}, f32[12,12]{1,0:T(8,128)}, u32[]{:S(2)}) copy-start(f32[12,12]{1,0:T(8,128)} %param.21) | copy-start | bytes 1732
  63.2 17.1 %copy-start.49 = (s32[12,12]{1,0:T(8,128)S(1)}, s32[12,12]{1,0:T(8,128)}, u32[]{:S(2)}) copy-start(s32[12,12]{1,0:T(8,128)} %param.19) | copy-start | bytes 1732
  63.2 41.6 %all-to-all-start.1 = ((bf16[32,2,9216]{2,1,0:T(2,128)(2,1)}), bf16[32,2,9216]{2,1,0:T(2,128)(2,1)}, u32[]{:S(2)}, u32[]{:S(2)}) async-start(bf16[32,2,9216]{2,1,0:T(2,128)(2,1)} %reshape.191), calls=%async_computation.1 | async-start | bytes 2359296 | tf_op jit(solution)/shard_map/all_to_all | solution.py:119
  82.5 0.7 copy-start.8
  114.8 1.7 copy-start.9
  114.8 1.7 copy-start.10
  126.6 7.3 %copy-start.44 = (f32[12,1,64]{2,1,0:T(1,128)S(1)}, f32[12,1,64]{2,1,0:T(1,128)}, u32[]{:S(2)}) copy-start(f32[12,1,64]{2,1,0:T(1,128)} %get-tuple-element.23) | copy-start | bytes 9220
  126.6 7.3 %copy-start.45 = (f32[12,1,64]{2,1,0:T(1,128)S(1)}, f32[12,1,64]{2,1,0:T(1,128)}, u32[]{:S(2)}) copy-start(f32[12,1,64]{2,1,0:T(1,128)} %get-tuple-element.24) | copy-start | bytes 9220
  126.6 7.9 %copy-start.42 = (f32[12,1,64]{2,1,0:T(1,128)S(1)}, f32[12,1,64]{2,1,0:T(1,128)}, u32[]{:S(2)}) copy-start(f32[12,1,64]{2,1,0:T(1,128)} %get-tuple-element.25) | copy-start | bytes 9220
  126.6 7.9 %copy-start.43 = (f32[12,1,64]{2,1,0:T(1,128)S(1)}, f32[12,1,64]{2,1,0:T(1,128)}, u32[]{:S(2)}) copy-start(f32[12,1,64]{2,1,0:T(1,128)} %get-tuple-element.26) | copy-start | bytes 9220
  126.6 8.5 %copy-start.40 = (f32[12,1,64]{2,1,0:T(1,128)S(1)}, f32[12,1,64]{2,1,0:T(1,128)}, u32[]{:S(2)}) copy-start(f32[12,1,64]{2,1,0:T(1,128)} %get-tuple-element.27) | copy-start | bytes 9220
  126.6 8.5 %copy-start.41 = (f32[12,1,64]{2,1,0:T(1,128)S(1)}, f32[12,1,64]{2,1,0:T(1,128)}, u32[]{:S(2)}) copy-start(f32[12,1,64]{2,1,0:T(1,128)} %get-tuple-element.28) | copy-start | bytes 9220
  126.6 9.1 %copy-start.38 = (f32[12,1,64]{2,1,0:T(1,128)S(1)}, f32[12,1,64]{2,1,0:T(1,128)}, u32[]{:S(2)}) copy-start(f32[12,1,64]{2,1,0:T(1,128)} %get-tuple-element.29) | copy-start | bytes 9220
  126.6 9.1 %copy-start.39 = (f32[12,1,64]{2,1,0:T(1,128)S(1)}, f32[12,1,64]{2,1,0:T(1,128)}, u32[]{:S(2)}) copy-start(f32[12,1,64]{2,1,0:T(1,128)} %get-tuple-element.30) | copy-start | bytes 9220
  126.6 9.7 %copy-start.36 = (f32[12,1,64]{2,1,0:T(1,128)S(1)}, f32[12,1,64]{2,1,0:T(1,128)}, u32[]{:S(2)}) copy-start(f32[12,1,64]{2,1,0:T(1,128)} %get-tuple-element.31) | copy-start | bytes 9220
  126.7 9.7 %copy-start.37 = (f32[12,1,64]{2,1,0:T(1,128)S(1)}, f32[12,1,64]{2,1,0:T(1,128)}, u32[]{:S(2)}) copy-start(f32[12,1,64]{2,1,0:T(1,128)} %get-tuple-element.32) | copy-start | bytes 9220
  126.7 10.3 %copy-start.34 = (f32[12,1,64]{2,1,0:T(1,128)S(1)}, f32[12,1,64]{2,1,0:T(1,128)}, u32[]{:S(2)}) copy-start(f32[12,1,64]{2,1,0:T(1,128)} %get-tuple-element.33) | copy-start | bytes 9220
  126.7 10.3 %copy-start.35 = (f32[12,1,64]{2,1,0:T(1,128)S(1)}, f32[12,1,64]{2,1,0:T(1,128)}, u32[]{:S(2)}) copy-start(f32[12,1,64]{2,1,0:T(1,128)} %get-tuple-element.34) | copy-start | bytes 9220
  126.7 14.1 %copy-start.46 = (f32[384]{0:T(512)S(1)}, f32[384]{0:T(512)}, u32[]{:S(2)}) copy-start(f32[384]{0:T(512)} %select_multiply_fusion) | copy-start | bytes 4612
  126.7 14.1 %copy-start.47 = (f32[384]{0:T(512)S(1)}, f32[384]{0:T(512)}, u32[]{:S(2)}) copy-start(f32[384]{0:T(512)} %fusion.83) | copy-start | bytes 4612
  126.7 36.8 %all-to-all-start.2 = ((bf16[32,2,9216]{2,1,0:T(2,128)(2,1)}), bf16[32,2,9216]{2,1,0:T(2,128)(2,1)S(1)}, u32[]{:S(2)}, u32[]{:S(2)}) async-start(bf16[32,2,9216]{2,1,0:T(2,128)(2,1)} %reshape.193), calls=%async_computation.2 | async-start | bytes 2359296 | tf_op jit(solution)/shard_map/all_to_all | solution.py:137
  167.9 5.9 %copy-start.2 = (f32[1,384,768]{2,1,0:T(8,128)S(1)}, f32[1,384,768]{2,1,0:T(8,128)}, u32[]{:S(2)}) copy-start(f32[1,384,768]{2,1,0:T(8,128)} %get-tuple-element.45) | copy-start | bytes 3538948
  167.9 5.9 %copy-start.3 = (f32[1,384,768]{2,1,0:T(8,128)S(1)}, f32[1,384,768]{2,1,0:T(8,128)}, u32[]{:S(2)}) copy-start(f32[1,384,768]{2,1,0:T(8,128)} %get-tuple-element.46) | copy-start | bytes 3538948
  173.8 1.3 copy-start.4
  176.3 9.6 %copy-start.32 = (f32[12,1,64]{2,1,0:T(1,128)S(1)}, f32[12,1,64]{2,1,0:T(1,128)}, u32[]{:S(2)}) copy-start(f32[12,1,64]{2,1,0:T(1,128)} %get-tuple-element.35) | copy-start | bytes 9220
  176.3 9.6 %copy-start.33 = (f32[12,1,64]{2,1,0:T(1,128)S(1)}, f32[12,1,64]{2,1,0:T(1,128)}, u32[]{:S(2)}) copy-start(f32[12,1,64]{2,1,0:T(1,128)} %get-tuple-element.40) | copy-start | bytes 9220
  176.7 11.0 %collective-permute-start = (bf16[2,772,64]{1,2,0:T(8,128)(2,1)S(1)}, bf16[2,772,64]{1,2,0:T(8,128)(2,1)S(1)}, u32[]{:S(2)}, u32[]{:S(2)}) collective-permute-start(bf16[2,772,64]{1,2,0:T(8,128)(2,1)S(1)} %get-tuple-element.12), channel_id=1, source_target_pairs={{0,8},{8,16},{16,24},{24,32},{32,40},{40,48},{48,56},{56,64},{64,7... | collective-permute-start | bytes 592904 | tf_op jit(solution)/shard_map/ppermute | solution.py:18
  178.6 10.8 %collective-permute-start.1 = (bf16[2,772,64]{1,2,0:T(8,128)(2,1)S(1)}, bf16[2,772,64]{1,2,0:T(8,128)(2,1)S(1)}, u32[]{:S(2)}, u32[]{:S(2)}) collective-permute-start(bf16[2,772,64]{1,2,0:T(8,128)(2,1)S(1)} %get-tuple-element.13), channel_id=1, source_target_pairs={{8,0},{16,8},{24,16},{32,24},{40,32},{48,40},{56,48},{64,56},{72,6... | collective-permute-start | bytes 592904 | tf_op jit(solution)/shard_map/ppermute | solution.py:21
  185.9 5.5 %copy-start.11 = (f32[12,64]{1,0:T(8,128)S(1)}, f32[12,64]{1,0:T(8,128)}, u32[]{:S(2)}) copy-start(f32[12,64]{1,0:T(8,128)} %get-tuple-element.49) | copy-start | bytes 9220
  185.9 5.5 %copy-start.12 = (f32[12,64]{1,0:T(8,128)S(1)}, f32[12,64]{1,0:T(8,128)}, u32[]{:S(2)}) copy-start(f32[12,64]{1,0:T(8,128)} %get-tuple-element.50) | copy-start | bytes 9220
  185.9 5.5 %copy-start.13 = (f32[12,64]{1,0:T(8,128)S(1)}, f32[12,64]{1,0:T(8,128)}, u32[]{:S(2)}) copy-start(f32[12,64]{1,0:T(8,128)} %get-tuple-element.51) | copy-start | bytes 9220
  185.9 5.5 %copy-start.14 = (f32[12,64]{1,0:T(8,128)S(1)}, f32[12,64]{1,0:T(8,128)}, u32[]{:S(2)}) copy-start(f32[12,64]{1,0:T(8,128)} %get-tuple-element.52) | copy-start | bytes 9220
  186.0 5.5 %copy-start.15 = (f32[12,64]{1,0:T(8,128)S(1)}, f32[12,64]{1,0:T(8,128)}, u32[]{:S(2)}) copy-start(f32[12,64]{1,0:T(8,128)} %get-tuple-element.53) | copy-start | bytes 9220
  186.0 5.5 %copy-start.16 = (f32[12,64]{1,0:T(8,128)S(1)}, f32[12,64]{1,0:T(8,128)}, u32[]{:S(2)}) copy-start(f32[12,64]{1,0:T(8,128)} %get-tuple-element.54) | copy-start | bytes 9220
  186.0 5.5 %copy-start.17 = (f32[12,64]{1,0:T(8,128)S(1)}, f32[12,64]{1,0:T(8,128)}, u32[]{:S(2)}) copy-start(f32[12,64]{1,0:T(8,128)} %get-tuple-element.55) | copy-start | bytes 9220
  186.0 5.5 %copy-start.18 = (f32[12,64]{1,0:T(8,128)S(1)}, f32[12,64]{1,0:T(8,128)}, u32[]{:S(2)}) copy-start(f32[12,64]{1,0:T(8,128)} %get-tuple-element.56) | copy-start | bytes 9220
  186.0 5.5 %copy-start.19 = (f32[12,64]{1,0:T(8,128)S(1)}, f32[12,64]{1,0:T(8,128)}, u32[]{:S(2)}) copy-start(f32[12,64]{1,0:T(8,128)} %get-tuple-element.57) | copy-start | bytes 9220
  186.0 5.5 %copy-start.20 = (f32[12,64]{1,0:T(8,128)S(1)}, f32[12,64]{1,0:T(8,128)}, u32[]{:S(2)}) copy-start(f32[12,64]{1,0:T(8,128)} %get-tuple-element.58) | copy-start | bytes 9220
  186.0 5.5 %copy-start.21 = (f32[12,64]{1,0:T(8,128)S(1)}, f32[12,64]{1,0:T(8,128)}, u32[]{:S(2)}) copy-start(f32[12,64]{1,0:T(8,128)} %get-tuple-element.59) | copy-start | bytes 9220
  186.0 5.5 %copy-start.22 = (f32[12,64]{1,0:T(8,128)S(1)}, f32[12,64]{1,0:T(8,128)}, u32[]{:S(2)}) copy-start(f32[12,64]{1,0:T(8,128)} %get-tuple-element.60) | copy-start | bytes 9220
  186.0 5.5 %copy-start.23 = (f32[12,64]{1,0:T(8,128)S(1)}, f32[12,64]{1,0:T(8,128)}, u32[]{:S(2)}) copy-start(f32[12,64]{1,0:T(8,128)} %get-tuple-element.61) | copy-start | bytes 9220
  186.0 5.5 %copy-start.24 = (f32[12,64]{1,0:T(8,128)S(1)}, f32[12,64]{1,0:T(8,128)}, u32[]{:S(2)}) copy-start(f32[12,64]{1,0:T(8,128)} %get-tuple-element.62) | copy-start | bytes 9220
  186.1 5.5 %copy-start.25 = (f32[12,64]{1,0:T(8,128)S(1)}, f32[12,64]{1,0:T(8,128)}, u32[]{:S(2)}) copy-start(f32[12,64]{1,0:T(8,128)} %get-tuple-element.63) | copy-start | bytes 9220
  186.1 5.5 %copy-start.26 = (f32[12,64]{1,0:T(8,128)S(1)}, f32[12,64]{1,0:T(8,128)}, u32[]{:S(2)}) copy-start(f32[12,64]{1,0:T(8,128)} %get-tuple-element.64) | copy-start | bytes 9220
  186.1 5.5 %copy-start.27 = (f32[12,64]{1,0:T(8,128)S(1)}, f32[12,64]{1,0:T(8,128)}, u32[]{:S(2)}) copy-start(f32[12,64]{1,0:T(8,128)} %get-tuple-element.65) | copy-start | bytes 9220
  186.1 5.5 %copy-start.28 = (f32[12,64]{1,0:T(8,128)S(1)}, f32[12,64]{1,0:T(8,128)}, u32[]{:S(2)}) copy-start(f32[12,64]{1,0:T(8,128)} %get-tuple-element.66) | copy-start | bytes 9220
  186.1 5.5 %copy-start.29 = (f32[12,64]{1,0:T(8,128)S(1)}, f32[12,64]{1,0:T(8,128)}, u32[]{:S(2)}) copy-start(f32[12,64]{1,0:T(8,128)} %get-tuple-element.67) | copy-start | bytes 9220
  186.1 5.5 %copy-start.30 = (f32[12,64]{1,0:T(8,128)S(1)}, f32[12,64]{1,0:T(8,128)}, u32[]{:S(2)}) copy-start(f32[12,64]{1,0:T(8,128)} %get-tuple-element.68) | copy-start | bytes 9220
  186.1 5.5 %copy-start.31 = (f32[12,1,64]{2,0,1:T(8,128)S(1)}, f32[12,1,64]{2,0,1:T(8,128)}, u32[]{:S(2)}) copy-start(f32[12,1,64]{2,0,1:T(8,128)} %copy.132) | copy-start | bytes 9220
  258.9 7.2 %copy-start.1 = (bf16[12,384,384]{2,1,0:T(8,128)(2,1)S(1)}, bf16[12,384,384]{2,1,0:T(8,128)(2,1)}, u32[]{:S(2)}) copy-start(bf16[12,384,384]{2,1,0:T(8,128)(2,1)} %param.16) | copy-start | bytes 10616836
where the time goes:
time: 268 us; the launch traced here: 266 us
  local copies, waits for them, and re-layouts  95.1 us (35%)
  waiting for transfers between devices  58.6 us (22%)
  other arithmetic  34.5 us (13%)
  starting transfers between devices  33.1 us (12%)
  blocking collectives  22.6 us (8%)
  matrix products  20.8 us (8%)
    unnamed x123, local copies, waits for them, and re-layouts  35.8 us
    all_to_all x1, blocking collectives, shards(): lax.all_to_all(spatial_part, 'lon', split_axis=1, concat_axis=2, tiled=True)  22.6 us
    all_to_all x1, waiting for transfers between devices, shards(): lax.all_to_all(field, 'lon', split_axis=2, concat_axis=1, tiled=True)  20.7 us
    all_to_all x1, waiting for transfers between devices, shards(): lax.all_to_all(weighted, 'lat', split_axis=0, concat_axis=1, tiled=True)  17.9 us
    all_to_all x1, waiting for transfers between devices, shards(): lax.all_to_all(synthesis, 'lat', split_axis=1, concat_axis=0, tiled=True)  16.7 us
    convert_element_type x1, other arithmetic, shards(): spatial_part = (wave.astype(jnp.float32) + conv).astype(jnp.bfloat16)  15.5 us
    all_to_all x1, starting transfers between devices, shards(): lax.all_to_all(weighted, 'lat', split_axis=0, concat_axis=1, tiled=True)  11.8 us
    convert_element_type x2, local copies, waits for them, and re-layouts, channel_mlp(): tokens = spatial.reshape(-1, channels).astype(jnp.float32)  10.8 us
  transfers between devices with their start and end apart: 5, of which 5 were waited for; matrix products, arithmetic and copies ran while one was open for 11% of the time, Pallas kernels for 0%

commit v1 on v0

--- a/solution.py
+++ b/solution.py
@@ -146,7 +146,12 @@
     padded = padded_2(cycle, (("lat", 0),), HALO)
     conv = convolve(padded, kernel, lat_rows, nlon)
     spatial_part = (wave.astype(jnp.float32) + conv).astype(jnp.bfloat16)
-    spatial = lax.all_to_all(spatial_part, "lon", split_axis=1, concat_axis=2, tiled=True)
+    spatial = jnp.concatenate(
+        lax.all_to_all(
+            jnp.stack(jnp.split(spatial_part, lax.axis_size("lon"), axis=1)), "lon", 0, 0
+        ),
+        axis=2,
+    )
     block_out = channel_mlp(spatial, field, norm_gain, w_in, b_in, w_out, b_out)
     return (block_out, spatial)
 

time: 268 us -> 254 us (0.948)
  local copies, waits for them, and re-layouts: 95.1 us -> 80.4 us
  blocking collectives: 22.6 us -> 26.6 us
  other arithmetic: 34.5 us -> 31.6 us
    unnamed x123 -> x128, local copies, waits for them, and re-layouts: 35.8 us -> 30.7 us
    all_to_all x1, blocking collectives: 22.6 us -> 26.6 us  [shards(): lax.all_to_all(jnp.stack(jnp.split(spatial_part, lax.axis_size('lon'), ax...]
    convert_element_type x1 -> x0, local copies, waits for them, and re-layouts: 3.92 us -> none  [shards(): spatial_part = (wave.astype(jnp.float32) + conv).astype(jnp.bfloat16)]
    all_to_all x1 -> x0, local copies, waits for them, and re-layouts: 3.87 us -> none  [shards(): lax.all_to_all(spatial_part, 'lon', split_axis=1, concat_axis=2, tiled=True)]
  transfers between devices with their start and end apart: 5 -> 5, of which waited for: 5 -> 5; matrix products, arithmetic and copies ran while one was open for 11% -> 12% of each run, Pallas kernels for 0% -> 0%
where the time goes in v1:
time: 254 us; the launch traced here: 253 us
  local copies, waits for them, and re-layouts  80.4 us (32%)
  waiting for transfers between devices  58.8 us (23%)
  starting transfers between devices  33.1 us (13%)
  other arithmetic  31.6 us (12%)
  blocking collectives  26.6 us (10%)
  matrix products  20.8 us (8%)
    unnamed x128, local copies, waits for them, and re-layouts  30.7 us
    all_to_all x1, blocking collectives, shards(): lax.all_to_all(jnp.stack(jnp.split(spatial_part, lax.axis_size('lon'), ax...  26.6 us
    all_to_all x1, waiting for transfers between devices, shards(): lax.all_to_all(field, 'lon', split_axis=2, concat_axis=1, tiled=True)  20.7 us
    all_to_all x1, waiting for transfers between devices, shards(): lax.all_to_all(weighted, 'lat', split_axis=0, concat_axis=1, tiled=True)  17.9 us
    all_to_all x1, waiting for transfers between devices, shards(): lax.all_to_all(synthesis, 'lat', split_axis=1, concat_axis=0, tiled=True)  16.9 us
    convert_element_type x1, other arithmetic, shards(): spatial_part = (wave.astype(jnp.float32) + conv).astype(jnp.bfloat16)  14.3 us
    all_to_all x1, starting transfers between devices, shards(): lax.all_to_all(weighted, 'lat', split_axis=0, concat_axis=1, tiled=True)  11.8 us
    convert_element_type x2, local copies, waits for them, and re-layouts, channel_mlp(): tokens = spatial.reshape(-1, channels).astype(jnp.float32)  8.88 us
  transfers between devices with their start and end apart: 5, of which 5 were waited for; matrix products, arithmetic and copies ran while one was open for 12% of the time, Pallas kernels for 0%

profile of v1, /device:TPU:16, one launch (start us, length us, event | category | flops | bytes accessed | tf_op | source)
XLA Modules:
  0.0 252.8 jit_solution(6298648503651847567)
XLA Ops:
  0.6 4.5 %copy.53 = bf16[12,96,512]{1,0,2:T(8,128)(2,1)} copy(bf16[12,96,512]{2,1,0:T(8,128)(2,1)} %param.14) | data formatting | bytes 2359296 | tf_op args[0]
  5.1 5.0 %all-to-all-start = ((bf16[12,96,512]{1,0,2:T(8,128)(2,1)}), bf16[12,96,512]{1,0,2:T(8,128)(2,1)}, u32[]{:S(2)}, u32[]{:S(2)}) async-start(bf16[12,96,512]{1,0,2:T(8,128)(2,1)} %copy.53), calls=%async_computation | async-start | bytes 4194304 | tf_op jit(solution)/shard_map/all_to_all | solution.py:107
  10.2 6.4 %multiply_negate_fusion = (f32[1,384,768]{2,1,0:T(8,128)}, f32[1,384,768]{2,1,0:T(8,128)}) fusion(), kind=kLoop, calls=%fused_computation.78 | loop fusion | flops 3538944 | bytes 2359296 | tf_op jit(solution)/shard_map/neg | solution.py:39
  16.5 20.7 %all-to-all-done = bf16[12,96,512]{1,0,2:T(8,128)(2,1)} async-done(((bf16[12,96,512]{1,0,2:T(8,128)(2,1)}), bf16[12,96,512]{1,0,2:T(8,128)(2,1)}, u32[]{:S(2)}, u32[]{:S(2)}) %all-to-all-start) | async-done | bytes 1179680 | tf_op jit(solution)/shard_map/all_to_all | solution.py:107
  37.2 3.8 %copy.55 = bf16[12,8,96,64]{2,1,3,0:T(8,128)(2,1)} copy(bf16[12,8,96,64]{2,0,3,1:T(8,128)(2,1)} %bitcast.4) | data formatting | bytes 2359296 | tf_op jit(solution)/shard_map/all_to_all | solution.py:107
  41.0 3.8 %reshape.188 = bf16[12,768,64,1]{1,2,0,3:T(8,128)(2,1)} reshape(bf16[12,8,96,64]{2,1,3,0:T(8,128)(2,1)} %copy.55) | data formatting | bytes 2359296 | tf_op jit(solution)/shard_map/all_to_all | solution.py:107
  44.8 3.2 %fusion.47 = f32[2,384,12,64]{1,3,2,0:T(8,128)S(1)} fusion(bf16[12,768,64,1]{1,2,0,3:T(8,128)(2,1)} %reshape.188, f32[1,384,768]{2,1,0:T(8,128)} %get-tuple-element.41, f32[1,384,768]{2,1,0:T(8,128)} %get-tuple-element.42), kind=kOutput, calls=%fused_computation.60 | convolution fusion | flops 908328960 | bytes 5898240 | tf_op jit(solution)/shard_map/tkc,rmk->rmtc/dot_general | solution.py:108
  48.1 2.2 fusion.40
  50.3 6.7 %copy.56 = bf16[384,12,2,64]{3,2,1,0:T(2,128)(2,1)} copy(bf16[384,12,2,64]{0,3,1,2:T(8,128)(2,1)} %fusion.40) | data formatting | bytes 2359296 | tf_op jit(solution)/shard_map/convert_element_type | solution.py:114
  56.9 6.3 %reshape.197 = bf16[32,2,9216]{2,1,0:T(2,128)(2,1)} reshape(bf16[384,12,2,64]{3,2,1,0:T(2,128)(2,1)} %copy.56) | data formatting | bytes 2359296
  63.2 11.8 %all-to-all-start.1 = ((bf16[32,2,9216]{2,1,0:T(2,128)(2,1)}), bf16[32,2,9216]{2,1,0:T(2,128)(2,1)}, u32[]{:S(2)}, u32[]{:S(2)}) async-start(bf16[32,2,9216]{2,1,0:T(2,128)(2,1)} %reshape.197), calls=%async_computation.1 | async-start | bytes 2359296 | tf_op jit(solution)/shard_map/all_to_all | solution.py:119
  75.0 2.0 constant_dynamic-slice_fusion
  77.0 1.7 copy.59
  78.7 1.7 copy.52
  80.3 1.0 fusion.81
  81.3 1.2 fusion.87
  82.6 0.7 copy-done.8
  83.2 0.7 fusion.103
  83.9 0.6 copy.129
  84.5 0.6 select_multiply_fusion
  85.1 0.6 fusion.90
  85.7 0.6 copy_bitcast_fusion.2
  86.3 0.6 copy_bitcast_fusion.4
  86.9 17.9 %all-to-all-done.1 = bf16[32,2,9216]{2,1,0:T(2,128)(2,1)} async-done(((bf16[32,2,9216]{2,1,0:T(2,128)(2,1)}), bf16[32,2,9216]{2,1,0:T(2,128)(2,1)}, u32[]{:S(2)}, u32[]{:S(2)}) %all-to-all-start.1) | async-done | bytes 1179680 | tf_op jit(solution)/shard_map/all_to_all | solution.py:119
  104.8 6.3 %reshape.198 = bf16[384,12,2,64]{3,2,1,0:T(2,128)(2,1)} reshape(bf16[32,2,9216]{2,1,0:T(2,128)(2,1)} %all-to-all-done.1) | data formatting | bytes 2359296
  111.1 3.7 %copy.57 = bf16[12,32,12,2,64]{4,3,2,1,0:T(2,128)(2,1)S(1)} copy(bf16[12,32,12,2,64]{4,3,2,0,1:T(2,128)(2,1)} %bitcast.172) | data formatting | bytes 2359296 | tf_op jit(solution)/shard_map/all_to_all | solution.py:119
  114.8 1.6 fusion.32
  116.4 0.4 subtract_convert_fusion.2
  116.8 2.0 fusion.42
  118.8 5.6 %copy.60 = bf16[12,384,2,64]{3,2,0,1:T(2,128)(2,1)S(1)} copy(bf16[12,384,2,64]{1,3,2,0:T(8,128)(2,1)} %fusion.42) | data formatting | bytes 2359296 | tf_op jit(solution)/shard_map/convert_element_type | solution.py:136
  124.4 2.2 reshape.199
  126.7 7.1 %all-to-all-start.2 = ((bf16[32,2,9216]{2,1,0:T(2,128)(2,1)}), bf16[32,2,9216]{2,1,0:T(2,128)(2,1)S(1)}, u32[]{:S(2)}, u32[]{:S(2)}) async-start(bf16[32,2,9216]{2,1,0:T(2,128)(2,1)} %reshape.199), calls=%async_computation.2 | async-start | bytes 2359296 | tf_op jit(solution)/shard_map/all_to_all | solution.py:137
  133.9 0.6 copy_bitcast_fusion.6
  134.5 0.6 copy_bitcast_fusion.8
  135.1 0.6 copy_bitcast_fusion.10
  135.7 0.6 copy_bitcast_fusion.12
  136.3 0.6 copy_bitcast_fusion.14
  136.9 0.6 copy_bitcast_fusion.16
  137.6 1.9 fusion.104
  139.4 0.6 copy_bitcast_fusion.18
  140.0 0.6 copy_bitcast_fusion.20
  140.6 6.0 %fusion.70 = (f32[1,384,768]{2,1,0:T(8,128)}, f32[1,384,768]{2,1,0:T(8,128)}) fusion(f32[384]{0:T(512)S(1)} %copy-done.46, f32[384]{0:T(512)S(1)} %copy-done.47), kind=kLoop, calls=%fused_computation.85 | loop fusion | flops 3244032 | bytes 2362368 | tf_op jit(solution)/shard_map/mul | solution.py:41
  146.6 16.9 %all-to-all-done.2 = bf16[32,2,9216]{2,1,0:T(2,128)(2,1)S(1)} async-done(((bf16[32,2,9216]{2,1,0:T(2,128)(2,1)}), bf16[32,2,9216]{2,1,0:T(2,128)(2,1)S(1)}, u32[]{:S(2)}, u32[]{:S(2)}) %all-to-all-start.2) | async-done | bytes 1179680 | tf_op jit(solution)/shard_map/all_to_all | solution.py:137
  163.5 1.4 reshape.200
  164.9 3.0 %copy.62 = bf16[32,12,12,2,64]{4,3,2,1,0:T(2,128)(2,1)} copy(bf16[32,12,12,2,64]{4,3,1,2,0:T(2,128)(2,1)S(1)} %bitcast.174) | data formatting | bytes 2359296 | tf_op jit(solution)/shard_map/all_to_all | solution.py:137
  167.9 5.9 %copy.63 = bf16[384,12,2,64]{0,3,2,1:T(8,128)(2,1)S(1)} copy(bf16[384,12,2,64]{3,2,1,0:T(2,128)(2,1)} %bitcast.175) | data formatting | bytes 2359296 | tf_op jit(solution)/shard_map/all_to_all | solution.py:137
  173.8 1.1 fusion.49
  175.1 1.2 fusion.41
  176.4 0.3 pad_maximum_fusion.7
  176.7 1.9 collective-permute-start
  178.6 7.3 %collective-permute-start.1 = (bf16[2,772,64]{1,2,0:T(8,128)(2,1)S(1)}, bf16[2,772,64]{1,2,0:T(8,128)(2,1)S(1)}, u32[]{:S(2)}, u32[]{:S(2)}) collective-permute-start(bf16[2,772,64]{1,2,0:T(8,128)(2,1)S(1)} %get-tuple-element.13), channel_id=1, source_target_pairs={{8,0},{16,8},{24,16},{32,24},{40,32},{48,40},{56,48},{64,56},{72,6... | collective-permute-start | bytes 592904 | tf_op jit(solution)/shard_map/ppermute | solution.py:21
  186.1 1.5 collective-permute-done
  187.6 1.8 collective-permute-done.1
  189.4 2.0 maximum_maximum_fusion
  191.6 14.3 %fusion.29 = bf16[12,768,64]{1,2,0:T(8,128)(2,1)S(1)} fusion(bf16[12,768,64]{1,2,0:T(8,128)(2,1)S(1)} %fusion.41, bf16[12,2,64]{1,2,0:T(8,128)(2,1)S(1)} %get-tuple-element.15, bf16[12,2,64]{1,2,0:T(8,128)(2,1)S(1)} %get-tuple-element.14, bf16[14,772,64]{1,2,0:T(8,128)(2,1)S(1)} %get-tuple-element.11, bf16[14,772,64]{1,2,0:T(8,128)(2,1)S(1)} %get-tuple-element.10, ...), kind=kLoop, calls=%fused_computation.42 | loop fusion | flops 51904512 | bytes 26035200 | tf_op jit(solution)/shard_map/convert_element_type | solution.py:148
  206.1 0.2 fusion.78
  207.0 26.6 %all_to_all.59 = bf16[8,12,96,64]{2,3,1,0:T(8,128)(2,1)S(1)} all-to-all(bf16[8,12,96,64]{2,3,1,0:T(8,128)(2,1)S(1)} %fusion.73), channel_id=1, replica_groups=mesh['lat'=32,'lon'=8] {'lon'}, dimensions={0} | all-to-all | bytes 2359296 | tf_op jit(solution)/shard_map/all_to_all | solution.py:150
  233.6 0.4 bitcast_convert_fusion
  234.0 3.8 %copy.65 = f32[12,96,8,64]{1,0,3,2:T(8,128)} copy(f32[12,96,8,64]{1,3,0,2:T(8,128)S(1)} %bitcast_convert_fusion) | data formatting | bytes 4718592 | tf_op jit(solution)/shard_map/convert_element_type | solution.py:70
  237.8 5.1 %reshape.185 = f32[1152,512]{0,1:T(8,128)} reshape(f32[12,96,8,64]{1,0,3,2:T(8,128)} %copy.65) | data formatting | bytes 4718592 | tf_op jit(solution)/shard_map/convert_element_type | solution.py:70
  242.9 0.3 convert_reduce_fusion
  243.3 0.5 multiply_reduce_fusion
  244.1 1.5 copy.67
  245.6 7.2 %fusion.13 = bf16[1152,512]{1,0:T(8,128)(2,1)} fusion(bf16[1024,512]{1,0:T(8,128)(2,1)} %param.26, bf16[1152,512]{1,0:T(8,128)(2,1)} %bitcast.178, f32[512]{0:T(512)} %param.27, bf16[512,1024]{1,0:T(8,128)(2,1)} %param.24, f32[1024]{0:T(1024)} %param.25, f32[1152,512]{0,1:T(8,128)} %reshape.185, f32[512]{0:T(512)} %param.23, f32[1152]{0:T(1024)S(1)} %rsqrt.12, ...), kind=kOutput, calls=%fused_computation.17 | convolution fusion | flops 2432434176 | bytes 6833152 | tf_op jit(solution)/shard_map/dot_general | solution.py:76
  (116 shorter events, 1.7 us)
Async XLA Ops:
  0.6 114.1 %copy-start = (bf16[12,384,384]{2,1,0:T(8,128)(2,1)S(1)}, bf16[12,384,384]{2,1,0:T(8,128)(2,1)}, u32[]{:S(2)}) copy-start(bf16[12,384,384]{2,1,0:T(8,128)(2,1)} %param.16) | copy-start | bytes 10616836
  5.1 32.1 %all-to-all-start = ((bf16[12,96,512]{1,0,2:T(8,128)(2,1)}), bf16[12,96,512]{1,0,2:T(8,128)(2,1)}, u32[]{:S(2)}, u32[]{:S(2)}) async-start(bf16[12,96,512]{1,0,2:T(8,128)(2,1)} %copy.53), calls=%async_computation | async-start | bytes 4194304 | tf_op jit(solution)/shard_map/all_to_all | solution.py:107
  44.8 3.3 %copy-start.5 = (f32[1,384,768]{2,1,0:T(8,128)S(1)}, f32[1,384,768]{2,1,0:T(8,128)}, u32[]{:S(2)}) copy-start(f32[1,384,768]{2,1,0:T(8,128)} %get-tuple-element.41) | copy-start | bytes 3538948
  44.8 3.3 %copy-start.6 = (f32[1,384,768]{2,1,0:T(8,128)S(1)}, f32[1,384,768]{2,1,0:T(8,128)}, u32[]{:S(2)}) copy-start(f32[1,384,768]{2,1,0:T(8,128)} %get-tuple-element.42) | copy-start | bytes 3538948
  44.8 3.3 %copy-start.7 = (bf16[12,768,64,1]{1,2,0,3:T(8,128)(2,1)S(1)}, bf16[12,768,64,1]{1,2,0,3:T(8,128)(2,1)}, u32[]{:S(2)}) copy-start(bf16[12,768,64,1]{1,2,0,3:T(8,128)(2,1)} %reshape.188) | copy-start | bytes 3538948
  44.8 3.3 %copy-start.50 = (f32[12]{0:T(128)S(1)}, f32[12]{0:T(128)}, u32[]{:S(2)}) copy-start(f32[12]{0:T(128)} %param.15) | copy-start | bytes 148
  63.2 17.1 %copy-start.48 = (f32[12,12]{1,0:T(8,128)S(1)}, f32[12,12]{1,0:T(8,128)}, u32[]{:S(2)}) copy-start(f32[12,12]{1,0:T(8,128)} %param.21) | copy-start | bytes 1732
  63.2 17.1 %copy-start.49 = (s32[12,12]{1,0:T(8,128)S(1)}, s32[12,12]{1,0:T(8,128)}, u32[]{:S(2)}) copy-start(s32[12,12]{1,0:T(8,128)} %param.19) | copy-start | bytes 1732
  63.2 41.6 %all-to-all-start.1 = ((bf16[32,2,9216]{2,1,0:T(2,128)(2,1)}), bf16[32,2,9216]{2,1,0:T(2,128)(2,1)}, u32[]{:S(2)}, u32[]{:S(2)}) async-start(bf16[32,2,9216]{2,1,0:T(2,128)(2,1)} %reshape.197), calls=%async_computation.1 | async-start | bytes 2359296 | tf_op jit(solution)/shard_map/all_to_all | solution.py:119
  82.5 0.7 copy-start.8
  114.8 1.7 copy-start.9
  114.8 1.7 copy-start.10
  126.6 7.3 %copy-start.44 = (f32[12,1,64]{2,1,0:T(1,128)S(1)}, f32[12,1,64]{2,1,0:T(1,128)}, u32[]{:S(2)}) copy-start(f32[12,1,64]{2,1,0:T(1,128)} %get-tuple-element.23) | copy-start | bytes 9220
  126.6 7.3 %copy-start.45 = (f32[12,1,64]{2,1,0:T(1,128)S(1)}, f32[12,1,64]{2,1,0:T(1,128)}, u32[]{:S(2)}) copy-start(f32[12,1,64]{2,1,0:T(1,128)} %get-tuple-element.24) | copy-start | bytes 9220
  126.6 7.9 %copy-start.42 = (f32[12,1,64]{2,1,0:T(1,128)S(1)}, f32[12,1,64]{2,1,0:T(1,128)}, u32[]{:S(2)}) copy-start(f32[12,1,64]{2,1,0:T(1,128)} %get-tuple-element.25) | copy-start | bytes 9220
  126.6 7.9 %copy-start.43 = (f32[12,1,64]{2,1,0:T(1,128)S(1)}, f32[12,1,64]{2,1,0:T(1,128)}, u32[]{:S(2)}) copy-start(f32[12,1,64]{2,1,0:T(1,128)} %get-tuple-element.26) | copy-start | bytes 9220
  126.6 8.5 %copy-start.40 = (f32[12,1,64]{2,1,0:T(1,128)S(1)}, f32[12,1,64]{2,1,0:T(1,128)}, u32[]{:S(2)}) copy-start(f32[12,1,64]{2,1,0:T(1,128)} %get-tuple-element.27) | copy-start | bytes 9220
  126.6 8.5 %copy-start.41 = (f32[12,1,64]{2,1,0:T(1,128)S(1)}, f32[12,1,64]{2,1,0:T(1,128)}, u32[]{:S(2)}) copy-start(f32[12,1,64]{2,1,0:T(1,128)} %get-tuple-element.28) | copy-start | bytes 9220
  126.6 9.1 %copy-start.38 = (f32[12,1,64]{2,1,0:T(1,128)S(1)}, f32[12,1,64]{2,1,0:T(1,128)}, u32[]{:S(2)}) copy-start(f32[12,1,64]{2,1,0:T(1,128)} %get-tuple-element.29) | copy-start | bytes 9220
  126.6 9.1 %copy-start.39 = (f32[12,1,64]{2,1,0:T(1,128)S(1)}, f32[12,1,64]{2,1,0:T(1,128)}, u32[]{:S(2)}) copy-start(f32[12,1,64]{2,1,0:T(1,128)} %get-tuple-element.30) | copy-start | bytes 9220
  126.6 9.7 %copy-start.36 = (f32[12,1,64]{2,1,0:T(1,128)S(1)}, f32[12,1,64]{2,1,0:T(1,128)}, u32[]{:S(2)}) copy-start(f32[12,1,64]{2,1,0:T(1,128)} %get-tuple-element.31) | copy-start | bytes 9220
  126.7 9.7 %copy-start.37 = (f32[12,1,64]{2,1,0:T(1,128)S(1)}, f32[12,1,64]{2,1,0:T(1,128)}, u32[]{:S(2)}) copy-start(f32[12,1,64]{2,1,0:T(1,128)} %get-tuple-element.32) | copy-start | bytes 9220
  126.7 10.3 %copy-start.34 = (f32[12,1,64]{2,1,0:T(1,128)S(1)}, f32[12,1,64]{2,1,0:T(1,128)}, u32[]{:S(2)}) copy-start(f32[12,1,64]{2,1,0:T(1,128)} %get-tuple-element.33) | copy-start | bytes 9220
  126.7 10.3 %copy-start.35 = (f32[12,1,64]{2,1,0:T(1,128)S(1)}, f32[12,1,64]{2,1,0:T(1,128)}, u32[]{:S(2)}) copy-start(f32[12,1,64]{2,1,0:T(1,128)} %get-tuple-element.34) | copy-start | bytes 9220
  126.7 13.9 %copy-start.46 = (f32[384]{0:T(512)S(1)}, f32[384]{0:T(512)}, u32[]{:S(2)}) copy-start(f32[384]{0:T(512)} %select_multiply_fusion) | copy-start | bytes 4612
  126.7 13.9 %copy-start.47 = (f32[384]{0:T(512)S(1)}, f32[384]{0:T(512)}, u32[]{:S(2)}) copy-start(f32[384]{0:T(512)} %fusion.90) | copy-start | bytes 4612
  126.7 36.8 %all-to-all-start.2 = ((bf16[32,2,9216]{2,1,0:T(2,128)(2,1)}), bf16[32,2,9216]{2,1,0:T(2,128)(2,1)S(1)}, u32[]{:S(2)}, u32[]{:S(2)}) async-start(bf16[32,2,9216]{2,1,0:T(2,128)(2,1)} %reshape.199), calls=%async_computation.2 | async-start | bytes 2359296 | tf_op jit(solution)/shard_map/all_to_all | solution.py:137
  167.9 5.9 %copy-start.2 = (f32[1,384,768]{2,1,0:T(8,128)S(1)}, f32[1,384,768]{2,1,0:T(8,128)}, u32[]{:S(2)}) copy-start(f32[1,384,768]{2,1,0:T(8,128)} %get-tuple-element.45) | copy-start | bytes 3538948
  167.9 5.9 %copy-start.3 = (f32[1,384,768]{2,1,0:T(8,128)S(1)}, f32[1,384,768]{2,1,0:T(8,128)}, u32[]{:S(2)}) copy-start(f32[1,384,768]{2,1,0:T(8,128)} %get-tuple-element.46) | copy-start | bytes 3538948
  173.8 1.3 copy-start.4
  176.3 9.6 %copy-start.32 = (f32[12,1,64]{2,1,0:T(1,128)S(1)}, f32[12,1,64]{2,1,0:T(1,128)}, u32[]{:S(2)}) copy-start(f32[12,1,64]{2,1,0:T(1,128)} %get-tuple-element.35) | copy-start | bytes 9220
  176.3 9.6 %copy-start.33 = (f32[12,1,64]{2,1,0:T(1,128)S(1)}, f32[12,1,64]{2,1,0:T(1,128)}, u32[]{:S(2)}) copy-start(f32[12,1,64]{2,1,0:T(1,128)} %get-tuple-element.40) | copy-start | bytes 9220
  176.7 11.0 %collective-permute-start = (bf16[2,772,64]{1,2,0:T(8,128)(2,1)S(1)}, bf16[2,772,64]{1,2,0:T(8,128)(2,1)S(1)}, u32[]{:S(2)}, u32[]{:S(2)}) collective-permute-start(bf16[2,772,64]{1,2,0:T(8,128)(2,1)S(1)} %get-tuple-element.12), channel_id=1, source_target_pairs={{0,8},{8,16},{16,24},{24,32},{32,40},{40,48},{48,56},{56,64},{64,7... | collective-permute-start | bytes 592904 | tf_op jit(solution)/shard_map/ppermute | solution.py:18
  178.6 10.8 %collective-permute-start.1 = (bf16[2,772,64]{1,2,0:T(8,128)(2,1)S(1)}, bf16[2,772,64]{1,2,0:T(8,128)(2,1)S(1)}, u32[]{:S(2)}, u32[]{:S(2)}) collective-permute-start(bf16[2,772,64]{1,2,0:T(8,128)(2,1)S(1)} %get-tuple-element.13), channel_id=1, source_target_pairs={{8,0},{16,8},{24,16},{32,24},{40,32},{48,40},{56,48},{64,56},{72,6... | collective-permute-start | bytes 592904 | tf_op jit(solution)/shard_map/ppermute | solution.py:21
  185.9 5.5 %copy-start.11 = (f32[12,64]{1,0:T(8,128)S(1)}, f32[12,64]{1,0:T(8,128)}, u32[]{:S(2)}) copy-start(f32[12,64]{1,0:T(8,128)} %get-tuple-element.49) | copy-start | bytes 9220
  185.9 5.5 %copy-start.12 = (f32[12,64]{1,0:T(8,128)S(1)}, f32[12,64]{1,0:T(8,128)}, u32[]{:S(2)}) copy-start(f32[12,64]{1,0:T(8,128)} %get-tuple-element.50) | copy-start | bytes 9220
  185.9 5.5 %copy-start.13 = (f32[12,64]{1,0:T(8,128)S(1)}, f32[12,64]{1,0:T(8,128)}, u32[]{:S(2)}) copy-start(f32[12,64]{1,0:T(8,128)} %get-tuple-element.51) | copy-start | bytes 9220
  185.9 5.5 %copy-start.14 = (f32[12,64]{1,0:T(8,128)S(1)}, f32[12,64]{1,0:T(8,128)}, u32[]{:S(2)}) copy-start(f32[12,64]{1,0:T(8,128)} %get-tuple-element.52) | copy-start | bytes 9220
  186.0 5.5 %copy-start.15 = (f32[12,64]{1,0:T(8,128)S(1)}, f32[12,64]{1,0:T(8,128)}, u32[]{:S(2)}) copy-start(f32[12,64]{1,0:T(8,128)} %get-tuple-element.53) | copy-start | bytes 9220
  186.0 5.5 %copy-start.16 = (f32[12,64]{1,0:T(8,128)S(1)}, f32[12,64]{1,0:T(8,128)}, u32[]{:S(2)}) copy-start(f32[12,64]{1,0:T(8,128)} %get-tuple-element.54) | copy-start | bytes 9220
  186.0 5.5 %copy-start.17 = (f32[12,64]{1,0:T(8,128)S(1)}, f32[12,64]{1,0:T(8,128)}, u32[]{:S(2)}) copy-start(f32[12,64]{1,0:T(8,128)} %get-tuple-element.55) | copy-start | bytes 9220
  186.0 5.5 %copy-start.18 = (f32[12,64]{1,0:T(8,128)S(1)}, f32[12,64]{1,0:T(8,128)}, u32[]{:S(2)}) copy-start(f32[12,64]{1,0:T(8,128)} %get-tuple-element.56) | copy-start | bytes 9220
  186.0 5.5 %copy-start.19 = (f32[12,64]{1,0:T(8,128)S(1)}, f32[12,64]{1,0:T(8,128)}, u32[]{:S(2)}) copy-start(f32[12,64]{1,0:T(8,128)} %get-tuple-element.57) | copy-start | bytes 9220
  186.0 5.5 %copy-start.20 = (f32[12,64]{1,0:T(8,128)S(1)}, f32[12,64]{1,0:T(8,128)}, u32[]{:S(2)}) copy-start(f32[12,64]{1,0:T(8,128)} %get-tuple-element.58) | copy-start | bytes 9220
  186.0 5.5 %copy-start.21 = (f32[12,64]{1,0:T(8,128)S(1)}, f32[12,64]{1,0:T(8,128)}, u32[]{:S(2)}) copy-start(f32[12,64]{1,0:T(8,128)} %get-tuple-element.59) | copy-start | bytes 9220
  186.0 5.5 %copy-start.22 = (f32[12,64]{1,0:T(8,128)S(1)}, f32[12,64]{1,0:T(8,128)}, u32[]{:S(2)}) copy-start(f32[12,64]{1,0:T(8,128)} %get-tuple-element.60) | copy-start | bytes 9220
  186.0 5.5 %copy-start.23 = (f32[12,64]{1,0:T(8,128)S(1)}, f32[12,64]{1,0:T(8,128)}, u32[]{:S(2)}) copy-start(f32[12,64]{1,0:T(8,128)} %get-tuple-element.61) | copy-start | bytes 9220
  186.0 5.5 %copy-start.24 = (f32[12,64]{1,0:T(8,128)S(1)}, f32[12,64]{1,0:T(8,128)}, u32[]{:S(2)}) copy-start(f32[12,64]{1,0:T(8,128)} %get-tuple-element.62) | copy-start | bytes 9220
  186.1 5.5 %copy-start.25 = (f32[12,64]{1,0:T(8,128)S(1)}, f32[12,64]{1,0:T(8,128)}, u32[]{:S(2)}) copy-start(f32[12,64]{1,0:T(8,128)} %get-tuple-element.63) | copy-start | bytes 9220
  186.1 5.5 %copy-start.26 = (f32[12,64]{1,0:T(8,128)S(1)}, f32[12,64]{1,0:T(8,128)}, u32[]{:S(2)}) copy-start(f32[12,64]{1,0:T(8,128)} %get-tuple-element.64) | copy-start | bytes 9220
  186.1 5.5 %copy-start.27 = (f32[12,64]{1,0:T(8,128)S(1)}, f32[12,64]{1,0:T(8,128)}, u32[]{:S(2)}) copy-start(f32[12,64]{1,0:T(8,128)} %get-tuple-element.65) | copy-start | bytes 9220
  186.1 5.5 %copy-start.28 = (f32[12,64]{1,0:T(8,128)S(1)}, f32[12,64]{1,0:T(8,128)}, u32[]{:S(2)}) copy-start(f32[12,64]{1,0:T(8,128)} %get-tuple-element.66) | copy-start | bytes 9220
  186.1 5.5 %copy-start.29 = (f32[12,64]{1,0:T(8,128)S(1)}, f32[12,64]{1,0:T(8,128)}, u32[]{:S(2)}) copy-start(f32[12,64]{1,0:T(8,128)} %get-tuple-element.67) | copy-start | bytes 9220
  186.1 5.5 %copy-start.30 = (f32[12,64]{1,0:T(8,128)S(1)}, f32[12,64]{1,0:T(8,128)}, u32[]{:S(2)}) copy-start(f32[12,64]{1,0:T(8,128)} %get-tuple-element.68) | copy-start | bytes 9220
  186.1 5.5 %copy-start.31 = (f32[12,1,64]{2,0,1:T(8,128)S(1)}, f32[12,1,64]{2,0,1:T(8,128)}, u32[]{:S(2)}) copy-start(f32[12,1,64]{2,0,1:T(8,128)} %copy.129) | copy-start | bytes 9220
  245.6 7.2 %copy-start.1 = (bf16[12,384,384]{2,1,0:T(8,128)(2,1)S(1)}, bf16[12,384,384]{2,1,0:T(8,128)(2,1)}, u32[]{:S(2)}) copy-start(bf16[12,384,384]{2,1,0:T(8,128)(2,1)} %param.16) | copy-start | bytes 10616836
